TPU v7x, 32 devices: a whole 2x2x4 slice. The times are simulated.
32 devices in a mesh: gx: 4 (over y, x), gy: 2 (over core), gz: 4 (over z).
Axes of the slice: x: 2, y: 2, z: 4, core: 2. Of those that a mesh axis runs over, the one named last changes fastest.
Arguments:
- positions: float32 [3, 8, 8, 8, 128], P(None, 'gx', 'gy', 'gz'), may hold values from 0 to 1
- type_ids: int32 [8, 8, 8, 128], P('gx', 'gy', 'gz'), may hold values from 0 to 1
- counts: int32 [8, 8, 8], P('gx', 'gy', 'gz'), may hold values from 64 to 128
- type_charge: float32 [2], replicated, may hold values from -1 to 1
- type_sigma: float32 [2], replicated, may hold values from 0.2 to 0.35
- type_epsilon: float32 [2], replicated, may hold values from 0.05 to 0.5
Outputs:
- forces: float32 [3, 8, 8, 8, 128], P(None, 'gx', 'gy', 'gz')
- totals: float32 [2], replicated
All inputs are finite; a program needn't handle non-finite values.
Results may differ from a plain program's by a relative error of at most 0.0003.
Values sent between devices are 32-bit elements; how exact they have to be, the bound alone decides.
A program may use at most 64 MiB of HBM per device.

v0:
```python
import jax
import jax.numpy as jnp
from jax import lax
from jax.sharding import PartitionSpec as P

soft_core = 0.09
corner_pairs = [
    (first_corner, second_corner)
    for first_corner in range(8)
    for second_corner in range(8)
    if first_corner & second_corner == 0 and first_corner <= second_corner
]


def passed_along(value, axis, steps):
    count = lax.axis_size(axis)
    pairs = [(source, (source + steps) % count) for source in range(count)]
    return lax.ppermute(value, axis, pairs)


def corner_of(which):
    return (which & 1, which >> 1 & 1, which >> 2 & 1)


def atom_table(positions, type_ids, counts, type_charge, type_sigma, type_epsilon):
    type_count = type_charge.shape[0]
    kinds_shape = (type_count, 1, 1, 1, 1)
    onehot = (
        type_ids[None] == jnp.arange(type_count, dtype=jnp.int32).reshape(kinds_shape)
    ).astype(jnp.float32)
    charge = jnp.sum(onehot * type_charge.reshape(kinds_shape), 0)
    sigma_atom = jnp.sum(onehot * type_sigma.reshape(kinds_shape), 0)
    depth_atom = jnp.sum(onehot * jnp.sqrt(type_epsilon).reshape(kinds_shape), 0)
    slots = lax.broadcasted_iota(jnp.int32, type_ids.shape, 3)
    occupied = (slots < counts[..., None]).astype(jnp.float32)
    return jnp.stack(
        [positions[0], positions[1], positions[2], charge, sigma_atom, depth_atom, occupied]
    )


def pair_terms(first, second, offset, selfpair):
    displace = second[:3, :, None, :] - first[:3, :, :, None] + offset[:, None, None, None]
    dist_sq = jnp.sum(displace * displace, 0)
    width_atoms = first.shape[-1]
    live_mask = first[6][:, :, None] * second[6][:, None, :] * (dist_sq < 1.0).astype(jnp.float32)
    if selfpair:
        ordered = (
            lax.broadcasted_iota(jnp.int32, (width_atoms, width_atoms), 0)
            < lax.broadcasted_iota(jnp.int32, (width_atoms, width_atoms), 1)
        ).astype(jnp.float32)
        live_mask = live_mask * ordered[None]
    sigma_pair = 0.5 * (first[4][:, :, None] + second[4][:, None, :])
    depth_pair = first[5][:, :, None] * second[5][:, None, :]
    coulomb = first[3][:, :, None] * second[3][:, None, :]
    soft_sq = dist_sq + soft_core
    inverse = lax.rsqrt(soft_sq)
    ratio_six = (sigma_pair * sigma_pair / soft_sq) ** 3
    ratio_twelve = ratio_six * ratio_six
    value_here = 4.0 * depth_pair * (ratio_twelve - ratio_six) + coulomb * inverse
    slope_here = (
        4.0 * depth_pair * (6.0 * ratio_six - 12.0 * ratio_twelve) - coulomb * inverse
    ) * inverse
    cut_sq = 1.0 + soft_core
    cut_len = cut_sq**0.5
    cut_six = (sigma_pair * sigma_pair / cut_sq) ** 3
    cut_twelve = cut_six * cut_six
    value_cut = 4.0 * depth_pair * (cut_twelve - cut_six) + coulomb / cut_len
    slope_cut = (
        4.0 * depth_pair * (6.0 * cut_six - 12.0 * cut_twelve) - coulomb / cut_len
    ) / cut_len
    energy = live_mask * (value_here - value_cut - (soft_sq * inverse - cut_len) * slope_cut)
    slope = live_mask * (slope_here - slope_cut) * inverse
    weighted = slope[None] * displace
    return (jnp.sum(weighted, 3), -jnp.sum(weighted, 2), jnp.sum(energy), jnp.sum(slope * dist_sq))


def per_device(positions, type_ids, counts, type_charge, type_sigma, type_epsilon):
    features = atom_table(positions, type_ids, counts, type_charge, type_sigma, type_epsilon)
    size_x, size_y, size_z, width_atoms = features.shape[1:]
    extended = jnp.concatenate([features, passed_along(features[:, :1], "gx", -1)], 1)
    extended = jnp.concatenate([extended, passed_along(extended[:, :, :1], "gy", -1)], 2)
    extended = jnp.concatenate([extended, passed_along(extended[:, :, :, :1], "gz", -1)], 3)
    cell_rows = size_x * size_y * size_z

    def slabs_of(which):
        shift_x, shift_y, shift_z = corner_of(which)
        view = extended[
            :, shift_x : shift_x + size_x, shift_y : shift_y + size_y, shift_z : shift_z + size_z
        ]
        return view.reshape((7, cell_rows, width_atoms))

    reaction = jnp.zeros((3, size_x + 1, size_y + 1, size_z + 1, width_atoms), jnp.float32)

    def deposit(reaction, force_rows, which):
        shift_x, shift_y, shift_z = corner_of(which)
        grid = force_rows.reshape((3, size_x, size_y, size_z, width_atoms))
        return reaction.at[
            :, shift_x : shift_x + size_x, shift_y : shift_y + size_y, shift_z : shift_z + size_z
        ].add(grid)

    energy = jnp.float32(0.0)
    virial = jnp.float32(0.0)
    for first_corner, second_corner in corner_pairs:
        offset = jnp.array(
            [float(a - b) for a, b in zip(corner_of(second_corner), corner_of(first_corner))],
            jnp.float32,
        )
        selfpair = first_corner == second_corner
        force_first, force_second, energies, virials = pair_terms(
            slabs_of(first_corner), slabs_of(second_corner), offset, selfpair
        )
        reaction = deposit(reaction, force_first, first_corner)
        reaction = deposit(reaction, force_second, second_corner)
        energy = energy + energies
        virial = virial + virials
    returned = passed_along(reaction[:, :, :, size_z:], "gz", 1)
    reaction = reaction[:, :, :, :size_z].at[:, :, :, :1].add(returned)
    returned = passed_along(reaction[:, :, size_y:], "gy", 1)
    reaction = reaction[:, :, :size_y].at[:, :, :1].add(returned)
    returned = passed_along(reaction[:, size_x:], "gx", 1)
    forces = reaction[:, :size_x].at[:, :1].add(returned)
    summed = lax.psum((energy, virial), ("gx", "gy", "gz"))
    normaliser = 1.0 / (
        size_x
        * lax.axis_size("gx")
        * size_y
        * lax.axis_size("gy")
        * size_z
        * lax.axis_size("gz")
        * width_atoms
    )
    totals = jnp.stack([summed[0], summed[1]]) * normaliser
    return (forces, totals)


def solution(mesh):
    in_specs = (
        P(None, "gx", "gy", "gz", None),
        P("gx", "gy", "gz", None),
        P("gx", "gy", "gz"),
        P(),
        P(),
        P(),
    )
    out_specs = (P(None, "gx", "gy", "gz", None), P())
    return jax.shard_map(
        per_device, mesh=mesh, in_specs=in_specs, out_specs=out_specs, check_vma=False
    )
```

profile of v0, /device:TPU:12, one launch (start us, length us, event | category | flops | bytes accessed | tf_op | source)
XLA Modules:
  0.0 161.7 jit_solution(2301316743114900686)
XLA Ops:
  0.7 0.7 copy.33
  1.4 0.7 sqrt.3
  2.1 0.7 constant_dynamic-update-slice_fusion.4
  2.8 0.8 copy.32
  3.6 0.8 select_reduce_fusion.2
  4.4 0.1 constant_dynamic-update-slice_fusion
  4.5 1.5 collective-permute-start
  6.0 0.1 lt.135
  6.1 0.1 fusion.332
  6.2 2.2 %collective-permute-done = f32[7,1,4,2,128]{4,3,2,1,0:T(2,128)S(1)} collective-permute-done((f32[7,1,4,2,128]{4,3,2,1,0:T(2,128)S(1)}, f32[7,1,4,2,128]{4,3,2,1,0:T(2,128)S(1)}, u32[]{:S(2)}, u32[]{:S(2)}) %collective-permute-start) | collective-permute-done | bytes 28704 | tf_op jit(solution)/shard_map/ppermute | solution.py:18
  8.4 0.1 collective-permute-start.1
  8.5 1.2 collective-permute-done.1
  9.8 0.5 collective-permute-start.2
  10.3 3.7 %collective-permute-done.2 = f32[7,3,5,1,128]{4,3,2,1,0:T(1,128)S(1)} collective-permute-done((f32[7,3,5,1,128]{4,3,2,1,0:T(1,128)S(1)}, f32[7,3,5,1,128]{4,3,2,1,0:T(1,128)S(1)}, u32[]{:S(2)}, u32[]{:S(2)}) %collective-permute-start.2) | collective-permute-done | bytes 53792 | tf_op jit(solution)/shard_map/ppermute | solution.py:18
  14.0 0.1 pad_maximum_fusion
  14.3 3.5 %multiply_reduce_fusion.1 = (f32[16,128,128]{2,1,0:T(8,128)S(1)}, f32[16,128,128]{2,1,0:T(8,128)S(1)}, f32[16,128,128]{2,1,0:T(8,128)S(1)}, f32[16,128,128]{2,1,0:T(8,128)S(1)}, f32[16,128,128]{2,1,0:T(8,128)S(1)}) fusion(f32[3]{0:T(128)S(1)} %copy-done.15, f32[3,16,128]{2,1,0:T(8,128)S(1)} %bitcast.72, f32[3,16,128]{2,1,0:T(8,128)S(1)} %bitcast.112, ...), kind=kLoop, calls=%fused_computation.10 | loop fusion | flops 14417920 | bytes 5341244 | tf_op jit(solution)/shard_map/reduce_sum | solution.py:43
  17.7 3.1 %fusion.132 = (f32[]{:T(128)}, f32[]{:T(128)}, f32[16,128,128]{2,1,0:T(8,128)S(1)}) fusion(f32[16,128,128]{2,1,0:T(8,128)S(1)} %get-tuple-element.475, f32[16,128]{1,0:T(8,128)S(1)} %bitcast.114, f32[16,128]{1,0:T(8,128)S(1)} %bitcast.138, f32[16,128]{1,0:T(8,128)S(1)} %bitcast.135, f32[16,128]{1,0:T(8,128)S(1)} %bitcast.132, f32[16,128]{1,0:T(8,128)S(1)} %bitcast.123, ...), kind=kLoop, calls=%fused_computation.314 | loop fusion | flops 13107198 | bytes 2162696 | tf_op jit(solution)/shard_map/reduce_sum | solution.py:74
  21.0 7.4 %fusion.160 = (f32[]{:T(128)}, f32[]{:T(128)}, f32[]{:T(128)}, f32[]{:T(128)}, f32[]{:T(128)}, /*index=5*/f32[]{:T(128)}, f32[16,128,128]{2,1,0:T(8,128)S(1)}, f32[16,128,128]{2,1,0:T(8,128)S(1)}, f32[16,128,128]{2,1,0:T(8,128)S(1)}) fusion(f32[16,128,128]{2,1,0:T(8,128)S(1)} %get-tuple-element.471, f32[16,128]{1,0:T(8,128)S(1)} %bitcast.124, ...), kind=kLoop, calls=%fused_computation.342 | loop fusion | flops 39321596 | bytes 6389784 | tf_op jit(solution)/shard_map/reduce_sum | solution.py:74
  28.4 8.2 %multiply_reduce_fusion = (f32[16,128,128]{2,1,0:T(8,128)S(1)}, f32[16,128,128]{2,1,0:T(8,128)S(1)}, f32[3,16,128]{2,1,0:T(8,128)}, f32[3,16,128]{2,1,0:T(8,128)...) fusion(f32[3]{0:T(128)S(1)} %copy-done.11, ...), kind=kLoop, calls=%fused_computation.5 | loop fusion | flops 29061120 | bytes 9756780 | tf_op jit(solution)/shard_map/reduce_sum | solution.py:43
  36.7 7.4 %fusion.146 = (f32[]{:T(128)}, f32[]{:T(128)}, f32[]{:T(128)}, f32[]{:T(128)}, f32[]{:T(128)}, /*index=5*/f32[]{:T(128)}, f32[16,128,128]{2,1,0:T(8,128)S(1)}, f32[16,128,128]{2,1,0:T(8,128)S(1)}, f32[16,128,128]{2,1,0:T(8,128)S(1)}) fusion(f32[16,128,128]{2,1,0:T(8,128)S(1)} %get-tuple-element.470, f32[16,128]{1,0:T(8,128)S(1)} %bitcast.115, ...), kind=kLoop, calls=%fused_computation.328 | loop fusion | flops 39321596 | bytes 6389784 | tf_op jit(solution)/shard_map/reduce_sum | solution.py:74
  44.1 4.8 %rsqrt_multiply_fusion.31 = (f32[16,128,128]{2,1,0:T(8,128)S(1)}, f32[16,128,128]{2,1,0:T(8,128)S(1)}, f32[16,128,128]{2,1,0:T(8,128)S(1)}) fusion(f32[16,128,128]{2,1,0:T(8,128)S(1)} %get-tuple-element.468, f32[16,128]{1,0:T(8,128)S(1)} %bitcast.147, f32[16,128]{1,0:T(8,128)S(1)} %bitcast.144, f32[16,128]{1,0:T(8,128)S(1)} %bitcast.141, ...), kind=kLoop, calls=%fused_computation.241 | loop fusion | flops 27525120 | bytes 6389760 | tf_op jit(solution)/shard_map/mul | solution.py:72
  48.9 10.2 %fusion.4 = (f32[3,16,128]{2,1,0:T(8,128)S(1)}, f32[3,16,128]{2,1,0:T(8,128)S(1)}, f32[16,128,128]{2,1,0:T(8,128)S(1)}, f32[3,16,128]{2,1,0:T(8,128)S(1)}, f32[3...) fusion(f32[16,128,128]{2,1,0:T(8,128)S(1)} %get-tuple-element.5, ...), kind=kLoop, calls=%fused_computation.8 | loop fusion | flops 31383552 | bytes 9879636 | tf_op jit(solution)/shard_map/reduce_sum | solution.py:74
  59.2 4.9 %fusion.167 = (f32[]{:T(128)}, f32[]{:T(128)}, f32[]{:T(128)}, f32[]{:T(128)}, f32[16,128,128]{2,1,0:T(8,128)S(1)}) fusion(f32[16,128,128]{2,1,0:T(8,128)S(1)} %get-tuple-element.459, f32[16,128]{1,0:T(8,128)S(1)} %bitcast.148, f32[16,128]{1,0:T(8,128)S(1)} %bitcast.145, f32[16,128]{1,0:T(8,128)S(1)} %bitcast.142, f32[16,128]{1,0:T(8,128)S(1)} %bitcast.130, ...), kind=kLoop, calls=%fused_computation.349 | loop fusion | flops 23855100 | bytes 4292624 | tf_op jit(solution)/shard_map/reduce_sum | solution.py:74
  64.1 7.0 %fusion.153 = (f32[]{:T(128)}, f32[]{:T(128)}, f32[]{:T(128)}, f32[]{:T(128)}, f32[]{:T(128)}, /*index=5*/f32[]{:T(128)}, f32[16,128,128]{2,1,0:T(8,128)S(1)}, f32[16,128,128]{2,1,0:T(8,128)S(1)}) fusion(f32[16,128,128]{2,1,0:T(8,128)S(1)} %get-tuple-element.460, f32[16,128]{1,0:T(8,128)S(1)} %bitcast.125, f32[16,128]{1,0:T(8,128)S(1)} %bitcast.122, ...), kind=kLoop, calls=%fused_computation.335 | loop fusion | flops 37224444 | bytes 6455320 | tf_op jit(solution)/shard_map/reduce_sum | solution.py:74
  71.1 4.6 %fusion.125 = (f32[]{:T(128)}, f32[]{:T(128)}, f32[]{:T(128)}, f32[]{:T(128)}, f32[16,128,128]{2,1,0:T(8,128)S(1)}) fusion(f32[16,128,128]{2,1,0:T(8,128)S(1)} %get-tuple-element.457, f32[16,128]{1,0:T(8,128)S(1)} %bitcast.192, f32[16,128]{1,0:T(8,128)S(1)} %bitcast.193, f32[16,128]{1,0:T(8,128)S(1)} %bitcast.194, f32[16,128]{1,0:T(8,128)S(1)} %bitcast.191, ...), kind=kLoop, calls=%fused_computation.307 | loop fusion | flops 23855100 | bytes 4292624 | tf_op jit(solution)/shard_map/reduce_sum | solution.py:74
  75.7 3.1 %fusion.22 = (f32[3,16,128]{2,1,0:T(8,128)S(1)}, f32[3,16,128]{2,1,0:T(8,128)S(1)}, f32[3,16,128]{2,1,0:T(8,128)S(1)}, f32[3,16,128]{2,1,0:T(8,128)S(1)}) fusion(f32[16,128,128]{2,1,0:T(8,128)S(1)} %get-tuple-element.489, f32[3,16,128]{2,1,0:T(8,128)S(1)} %bitcast.107, f32[3,16,128]{2,1,0:T(8,128)S(1)} %bitcast.82, f32[16,128,128]{2,1,0:T(8,128)S(1)} %get-tuple-element.497), kind=kLoop, calls=%fused_computation.38 | loop fusion | flops 7053312 | bytes 2244608 | tf_op jit(solution)/shard_map/reduce_sum | solution.py:74
  78.9 0.6 neg.108
  79.8 0.2 scatter-add.119
  80.0 0.8 fusion.319
  80.8 0.8 slice_add_fusion.16
  81.5 0.2 scatter-add.121
  81.8 0.2 scatter-add.125
  82.1 0.2 scatter-add.129
  82.4 5.0 %fusion.10 = (f32[3,16,128]{2,1,0:T(8,128)S(1)}, f32[3,16,128]{2,1,0:T(8,128)S(1)}, f32[3,16,128]{2,1,0:T(8,128)S(1)}, f32[3,16,128]{2,1,0:T(8,128)S(1)}, f32[3,...) fusion(f32[16,128,128]{2,1,0:T(8,128)S(1)} %get-tuple-element.496, f32[3]{0:T(128)S(1)} %copy-done.12, ...), kind=kLoop, calls=%fused_computation.18 | loop fusion | flops 11759616 | bytes 3366948 | tf_op jit(solution)/shard_map/reduce_sum | solution.py:74
  87.5 0.2 scatter-add.135
  87.8 0.2 scatter-add.139
  88.1 0.2 scatter-add.141
  88.4 0.2 scatter-add.145
  88.7 0.2 scatter-add.149
  89.0 1.6 %collective-permute-start.3 = (f32[3,3,5,1,128]{4,3,2,1,0:T(1,128)S(1)}, f32[3,3,5,1,128]{4,3,2,1,0:T(1,128)S(1)}, u32[]{:S(2)}, u32[]{:S(2)}) collective-permute-start(f32[3,3,5,1,128]{4,3,2,1,0:T(1,128)S(1)} %slice.1705), channel_id=1, source_target_pairs={{0,1},{1,2},{2,3},{3,0},{4,5},{5,6},{6,7},{7,4},{8,9},{9,10},{10,1... | collective-permute-start | bytes 69128 | tf_op jit(solution)/shard_map/ppermute | solution.py:18
  90.6 2.2 %collective-permute-done.3 = f32[3,3,5,1,128]{4,3,2,1,0:T(1,128)S(1)} collective-permute-done((f32[3,3,5,1,128]{4,3,2,1,0:T(1,128)S(1)}, f32[3,3,5,1,128]{4,3,2,1,0:T(1,128)S(1)}, u32[]{:S(2)}, u32[]{:S(2)}) %collective-permute-start.3) | collective-permute-done | bytes 23072 | tf_op jit(solution)/shard_map/ppermute | solution.py:18
  92.8 0.1 scatter-add.150
  93.0 0.1 collective-permute-start.4
  110.7 45.7 %all-reduce.1 = (f32[1]{0:T(128)}, f32[1]{0:T(128)}) all-reduce(f32[1]{0:T(128)} %bitcast.71, f32[1]{0:T(128)} %bitcast.70), channel_id=1, replica_groups=mesh['gx'=4,'gy'=2,'gz'=4] {'gx','gy','gz'}, use_global_device_ids=true, to_apply=%region_74.0 | all-reduce | flops 2 | bytes 16 | tf_op jit(solution)/shard_map/psum | solution.py:122
  156.4 0.6 collective-permute-start.5
  157.0 1.9 %maximum_multiply_fusion = f32[2]{0:T(128)} fusion(f32[1]{0:T(128)} %get-tuple-element.485, f32[1]{0:T(128)} %get-tuple-element.486), kind=kLoop, calls=%fused_computation.665 | loop fusion | flops 4 | bytes 16 | tf_op jit(solution)/shard_map/mul | solution.py:132
  159.0 2.1 %collective-permute-done.5 = f32[3,1,4,2,128]{4,3,2,1,0:T(2,128)S(1)} collective-permute-done((f32[3,1,4,2,128]{4,3,2,1,0:T(2,128)S(1)}, f32[3,1,4,2,128]{4,3,2,1,0:T(2,128)S(1)}, u32[]{:S(2)}, u32[]{:S(2)}) %collective-permute-start.5) | collective-permute-done | bytes 12320 | tf_op jit(solution)/shard_map/ppermute | solution.py:18
  161.1 0.6 copy-done.3
  (100 shorter events, 1.3 us)
Async XLA Ops:
  0.6 13.6 %copy-start.5 = (f32[3]{0:T(128)S(1)}, f32[3]{0:T(128)}, u32[]{:S(2)}) copy-start(f32[3]{0:T(128)} %constant.879.clone) | copy-start | bytes 40
  0.6 13.6 %copy-start.13 = (f32[3]{0:T(128)S(1)}, f32[3]{0:T(128)}, u32[]{:S(2)}) copy-start(f32[3]{0:T(128)} %constant.880.clone) | copy-start | bytes 40
  0.7 13.6 %copy-start.14 = (f32[3]{0:T(128)S(1)}, f32[3]{0:T(128)}, u32[]{:S(2)}) copy-start(f32[3]{0:T(128)} %constant.883.clone) | copy-start | bytes 40
  0.7 13.6 %copy-start.6 = (f32[3]{0:T(128)S(1)}, f32[3]{0:T(128)}, u32[]{:S(2)}) copy-start(f32[3]{0:T(128)} %constant.886.clone) | copy-start | bytes 40
  0.7 13.6 %copy-start.15 = (f32[3]{0:T(128)S(1)}, f32[3]{0:T(128)}, u32[]{:S(2)}) copy-start(f32[3]{0:T(128)} %constant.890.clone) | copy-start | bytes 40
  0.7 13.6 %copy-start = (f32[3,2,4,2,128]{4,3,2,1,0:T(2,128)S(1)}, f32[3,2,4,2,128]{4,3,2,1,0:T(2,128)}, u32[]{:S(2)}) copy-start(f32[3,2,4,2,128]{4,3,2,1,0:T(2,128)} %param.82) | copy-start | bytes 73732
  4.5 3.9 %collective-permute-start = (f32[7,1,4,2,128]{4,3,2,1,0:T(2,128)S(1)}, f32[7,1,4,2,128]{4,3,2,1,0:T(2,128)S(1)}, u32[]{:S(2)}, u32[]{:S(2)}) collective-permute-start(f32[7,1,4,2,128]{4,3,2,1,0:T(2,128)S(1)} %slice.1661), channel_id=1, source_target_pairs={{0,24},{8,0},{16,8},{24,16},{1,25},{9,1},{17,9},{25,17},{2,26},{10... | collective-permute-start | bytes 86024 | tf_op jit(solution)/shard_map/ppermute | solution.py:18
  8.4 1.3 collective-permute-start.1
  9.8 4.2 %collective-permute-start.2 = (f32[7,3,5,1,128]{4,3,2,1,0:T(1,128)S(1)}, f32[7,3,5,1,128]{4,3,2,1,0:T(1,128)S(1)}, u32[]{:S(2)}, u32[]{:S(2)}) collective-permute-start(f32[7,3,5,1,128]{4,3,2,1,0:T(1,128)S(1)} %slice.1680), channel_id=1, source_target_pairs={{0,3},{1,0},{2,1},{3,2},{4,7},{5,4},{6,5},{7,6},{8,11},{9,8},{10,9... | collective-permute-start | bytes 161288 | tf_op jit(solution)/shard_map/ppermute | solution.py:18
  20.9 7.5 %copy-start.7 = (f32[3]{0:T(128)S(1)}, f32[3]{0:T(128)}, u32[]{:S(2)}) copy-start(f32[3]{0:T(128)} %constant.881.clone) | copy-start | bytes 40
  20.9 7.5 %copy-start.8 = (f32[3]{0:T(128)S(1)}, f32[3]{0:T(128)}, u32[]{:S(2)}) copy-start(f32[3]{0:T(128)} %constant.882.clone) | copy-start | bytes 40
  20.9 7.5 %copy-start.9 = (f32[3]{0:T(128)S(1)}, f32[3]{0:T(128)}, u32[]{:S(2)}) copy-start(f32[3]{0:T(128)} %constant.884.clone) | copy-start | bytes 40
  20.9 7.4 %copy-start.10 = (f32[3]{0:T(128)S(1)}, f32[3]{0:T(128)}, u32[]{:S(2)}) copy-start(f32[3]{0:T(128)} %constant.888.clone) | copy-start | bytes 40
  21.0 7.4 %copy-start.11 = (f32[3]{0:T(128)S(1)}, f32[3]{0:T(128)}, u32[]{:S(2)}) copy-start(f32[3]{0:T(128)} %constant.891.clone) | copy-start | bytes 40
  21.0 7.4 %copy-start.12 = (f32[3]{0:T(128)S(1)}, f32[3]{0:T(128)}, u32[]{:S(2)}) copy-start(f32[3]{0:T(128)} %constant.889.clone) | copy-start | bytes 40
  44.1 4.8 %copy-start.4 = (f32[3]{0:T(128)S(1)}, f32[3]{0:T(128)}, u32[]{:S(2)}) copy-start(f32[3]{0:T(128)} %constant.887.clone) | copy-start | bytes 40
  82.3 6.0 %copy-start.1 = (f32[3,16,128]{2,1,0:T(8,128)S(1)}, f32[3,16,128]{2,1,0:T(8,128)}, u32[]{:S(2)}) copy-start(f32[3,16,128]{2,1,0:T(8,128)} %get-tuple-element.462) | copy-start | bytes 73732
  82.3 6.0 %copy-start.2 = (f32[3,16,128]{2,1,0:T(8,128)S(1)}, f32[3,16,128]{2,1,0:T(8,128)}, u32[]{:S(2)}) copy-start(f32[3,16,128]{2,1,0:T(8,128)} %get-tuple-element.461) | copy-start | bytes 73732
  89.0 3.9 %collective-permute-start.3 = (f32[3,3,5,1,128]{4,3,2,1,0:T(1,128)S(1)}, f32[3,3,5,1,128]{4,3,2,1,0:T(1,128)S(1)}, u32[]{:S(2)}, u32[]{:S(2)}) collective-permute-start(f32[3,3,5,1,128]{4,3,2,1,0:T(1,128)S(1)} %slice.1705), channel_id=1, source_target_pairs={{0,1},{1,2},{2,3},{3,0},{4,5},{5,6},{6,7},{7,4},{8,9},{9,10},{10,1... | collective-permute-start | bytes 69128 | tf_op jit(solution)/shard_map/ppermute | solution.py:18
  93.0 63.4 %collective-permute-start.4 = (f32[3,3,1,2,128]{4,3,2,1,0:T(2,128)S(1)}, f32[3,3,1,2,128]{4,3,2,1,0:T(2,128)S(1)}, u32[]{:S(2)}, u32[]{:S(2)}) collective-permute-start(f32[3,3,1,2,128]{4,3,2,1,0:T(2,128)S(1)} %slice.1708), channel_id=1, source_target_pairs={{0,4},{4,0},{1,5},{5,1},{2,6},{6,2},{3,7},{7,3},{8,12},{12,8},{9,1... | collective-permute-start | bytes 27656 | tf_op jit(solution)/shard_map/ppermute | solution.py:18
  156.4 4.6 %collective-permute-start.5 = (f32[3,1,4,2,128]{4,3,2,1,0:T(2,128)S(1)}, f32[3,1,4,2,128]{4,3,2,1,0:T(2,128)S(1)}, u32[]{:S(2)}, u32[]{:S(2)}) collective-permute-start(f32[3,1,4,2,128]{4,3,2,1,0:T(2,128)S(1)} %slice.1711), channel_id=1, source_target_pairs={{0,8},{8,16},{16,24},{24,0},{1,9},{9,17},{17,25},{25,1},{2,10},{10... | collective-permute-start | bytes 36872 | tf_op jit(solution)/shard_map/ppermute | solution.py:18
  161.1 0.6 copy-start.3
where the time goes:
time: 162 us
  other arithmetic  75.3 us (46%)
  blocking collectives  45.7 us (28%)
  between operations  19 us (12%)
  waiting for transfers between devices  11.4 us (7%)
  local copies, waits for them, and re-layouts  5.94 us (4%)
  starting transfers between devices  4.34 us (3%)
    psum x1, blocking collectives, per_device(): summed = lax.psum((energy, virial), ('gx', 'gy', 'gz'))  45.7 us
    reduce_sum x6, other arithmetic, pair_terms(): jnp.sum(energy)  34.4 us
    reduce_sum x3, other arithmetic, pair_terms(): jnp.sum(weighted, 2)  18.3 us
    reduce_sum x2, other arithmetic, pair_terms(): dist_sq = jnp.sum(displace * displace, 0)  11.7 us
    ppermute x6, waiting for transfers between devices, passed_along(): return lax.ppermute(value, axis, pairs)  11.4 us
    mul x1, other arithmetic, pair_terms(): slope = live_mask * (slope_here - slope_cut) * inverse  4.8 us
    ppermute x6, starting transfers between devices, passed_along(): return lax.ppermute(value, axis, pairs)  4.34 us
  transfers between devices with their start and end apart: 6, of which 5 were waited for; matrix products, arithmetic and copies ran while one was open for 1% of the time, Pallas kernels for 0%

commit v1 on v0

--- a/solution.py
+++ b/solution.py
@@ -119,7 +119,7 @@
     reaction = reaction[:, :, :size_y].at[:, :, :1].add(returned)
     returned = passed_along(reaction[:, size_x:], "gx", 1)
     forces = reaction[:, :size_x].at[:, :1].add(returned)
-    summed = lax.psum((energy, virial), ("gx", "gy", "gz"))
+    summed = lax.psum(lax.psum((energy, virial), ("gy", "gz")), "gx")
     normaliser = 1.0 / (
         size_x
         * lax.axis_size("gx")

time: 162 us -> 149 us (0.920)
  the two profiles are of different devices: /device:TPU:12 before, /device:TPU:0 now
where the time goes in v1:
time: 149 us; the launch traced here: 148 us
  other arithmetic  74.8 us (50%)
  blocking collectives  27.7 us (19%)
  between operations  19 us (13%)
  waiting for transfers between devices  12.5 us (8%)
  starting transfers between devices  8.2 us (6%)
  local copies, waits for them, and re-layouts  5.94 us (4%)
    reduce_sum x6, other arithmetic, pair_terms(): jnp.sum(energy)  34.4 us
    psum x2, blocking collectives, per_device(): summed = lax.psum(lax.psum((energy, virial), ('gy', 'gz')), 'gx')  27.7 us
    reduce_sum x3, other arithmetic, pair_terms(): jnp.sum(weighted, 2)  17.9 us
    ppermute x6, waiting for transfers between devices, passed_along(): return lax.ppermute(value, axis, pairs)  12.5 us
    reduce_sum x2, other arithmetic, pair_terms(): dist_sq = jnp.sum(displace * displace, 0)  11.7 us
    ppermute x6, starting transfers between devices, passed_along(): return lax.ppermute(value, axis, pairs)  8.2 us
    mul x1, other arithmetic, pair_terms(): slope = live_mask * (slope_here - slope_cut) * inverse  4.81 us
  transfers between devices with their start and end apart: 6, of which 5 were waited for; matrix products, arithmetic and copies ran while one was open for 1% of the time, Pallas kernels for 0%

profile of v1, /device:TPU:0, one launch (start us, length us, event | category | flops | bytes accessed | tf_op | source)
XLA Modules:
  0.0 148.2 jit_solution(9565236788531744549)
XLA Ops:
  0.7 0.7 copy.33
  1.4 0.7 sqrt.3
  2.1 0.7 constant_dynamic-update-slice_fusion.4
  2.8 0.8 copy.32
  3.6 0.8 select_reduce_fusion.2
  4.4 0.1 constant_dynamic-update-slice_fusion
  4.5 4.0 %collective-permute-start = (f32[7,1,4,2,128]{4,3,2,1,0:T(2,128)S(1)}, f32[7,1,4,2,128]{4,3,2,1,0:T(2,128)S(1)}, u32[]{:S(2)}, u32[]{:S(2)}) collective-permute-start(f32[7,1,4,2,128]{4,3,2,1,0:T(2,128)S(1)} %slice.1661), channel_id=1, source_target_pairs={{0,24},{8,0},{16,8},{24,16},{1,25},{9,1},{17,9},{25,17},{2,26},{10... | collective-permute-start | bytes 86024 | tf_op jit(solution)/shard_map/ppermute | solution.py:18
  8.5 0.1 lt.135
  8.6 0.1 fusion.332
  8.7 1.3 collective-permute-done
  10.1 0.1 collective-permute-start.1
  10.2 1.2 collective-permute-done.1
  11.4 3.7 %collective-permute-start.2 = (f32[7,3,5,1,128]{4,3,2,1,0:T(1,128)S(1)}, f32[7,3,5,1,128]{4,3,2,1,0:T(1,128)S(1)}, u32[]{:S(2)}, u32[]{:S(2)}) collective-permute-start(f32[7,3,5,1,128]{4,3,2,1,0:T(1,128)S(1)} %slice.1680), channel_id=1, source_target_pairs={{0,3},{1,0},{2,1},{3,2},{4,7},{5,4},{6,5},{7,6},{8,11},{9,8},{10,9... | collective-permute-start | bytes 161288 | tf_op jit(solution)/shard_map/ppermute | solution.py:18
  15.1 1.8 %collective-permute-done.2 = f32[7,3,5,1,128]{4,3,2,1,0:T(1,128)S(1)} collective-permute-done((f32[7,3,5,1,128]{4,3,2,1,0:T(1,128)S(1)}, f32[7,3,5,1,128]{4,3,2,1,0:T(1,128)S(1)}, u32[]{:S(2)}, u32[]{:S(2)}) %collective-permute-start.2) | collective-permute-done | bytes 53792 | tf_op jit(solution)/shard_map/ppermute | solution.py:18
  16.9 0.1 pad_maximum_fusion
  17.1 3.5 %multiply_reduce_fusion.1 = (f32[16,128,128]{2,1,0:T(8,128)S(1)}, f32[16,128,128]{2,1,0:T(8,128)S(1)}, f32[16,128,128]{2,1,0:T(8,128)S(1)}, f32[16,128,128]{2,1,0:T(8,128)S(1)}, f32[16,128,128]{2,1,0:T(8,128)S(1)}) fusion(f32[3]{0:T(128)S(1)} %copy-done.15, f32[3,16,128]{2,1,0:T(8,128)S(1)} %bitcast.72, f32[3,16,128]{2,1,0:T(8,128)S(1)} %bitcast.112, ...), kind=kLoop, calls=%fused_computation.10 | loop fusion | flops 14417920 | bytes 5341244 | tf_op jit(solution)/shard_map/reduce_sum | solution.py:43
  20.7 3.1 %fusion.132 = (f32[]{:T(128)}, f32[]{:T(128)}, f32[16,128,128]{2,1,0:T(8,128)S(1)}) fusion(f32[16,128,128]{2,1,0:T(8,128)S(1)} %get-tuple-element.475, f32[16,128]{1,0:T(8,128)S(1)} %bitcast.114, f32[16,128]{1,0:T(8,128)S(1)} %bitcast.138, f32[16,128]{1,0:T(8,128)S(1)} %bitcast.135, f32[16,128]{1,0:T(8,128)S(1)} %bitcast.132, f32[16,128]{1,0:T(8,128)S(1)} %bitcast.123, ...), kind=kLoop, calls=%fused_computation.314 | loop fusion | flops 13107198 | bytes 2162696 | tf_op jit(solution)/shard_map/reduce_sum | solution.py:74
  23.9 7.4 %fusion.160 = (f32[]{:T(128)}, f32[]{:T(128)}, f32[]{:T(128)}, f32[]{:T(128)}, f32[]{:T(128)}, /*index=5*/f32[]{:T(128)}, f32[16,128,128]{2,1,0:T(8,128)S(1)}, f32[16,128,128]{2,1,0:T(8,128)S(1)}, f32[16,128,128]{2,1,0:T(8,128)S(1)}) fusion(f32[16,128,128]{2,1,0:T(8,128)S(1)} %get-tuple-element.471, f32[16,128]{1,0:T(8,128)S(1)} %bitcast.124, ...), kind=kLoop, calls=%fused_computation.342 | loop fusion | flops 39321596 | bytes 6389784 | tf_op jit(solution)/shard_map/reduce_sum | solution.py:74
  31.3 8.2 %multiply_reduce_fusion = (f32[16,128,128]{2,1,0:T(8,128)S(1)}, f32[16,128,128]{2,1,0:T(8,128)S(1)}, f32[3,16,128]{2,1,0:T(8,128)}, f32[3,16,128]{2,1,0:T(8,128)...) fusion(f32[3]{0:T(128)S(1)} %copy-done.11, ...), kind=kLoop, calls=%fused_computation.5 | loop fusion | flops 29061120 | bytes 9756780 | tf_op jit(solution)/shard_map/reduce_sum | solution.py:43
  39.6 7.4 %fusion.146 = (f32[]{:T(128)}, f32[]{:T(128)}, f32[]{:T(128)}, f32[]{:T(128)}, f32[]{:T(128)}, /*index=5*/f32[]{:T(128)}, f32[16,128,128]{2,1,0:T(8,128)S(1)}, f32[16,128,128]{2,1,0:T(8,128)S(1)}, f32[16,128,128]{2,1,0:T(8,128)S(1)}) fusion(f32[16,128,128]{2,1,0:T(8,128)S(1)} %get-tuple-element.470, f32[16,128]{1,0:T(8,128)S(1)} %bitcast.115, ...), kind=kLoop, calls=%fused_computation.328 | loop fusion | flops 39321596 | bytes 6389784 | tf_op jit(solution)/shard_map/reduce_sum | solution.py:74
  47.0 4.8 %rsqrt_multiply_fusion.31 = (f32[16,128,128]{2,1,0:T(8,128)S(1)}, f32[16,128,128]{2,1,0:T(8,128)S(1)}, f32[16,128,128]{2,1,0:T(8,128)S(1)}) fusion(f32[16,128,128]{2,1,0:T(8,128)S(1)} %get-tuple-element.468, f32[16,128]{1,0:T(8,128)S(1)} %bitcast.147, f32[16,128]{1,0:T(8,128)S(1)} %bitcast.144, f32[16,128]{1,0:T(8,128)S(1)} %bitcast.141, ...), kind=kLoop, calls=%fused_computation.241 | loop fusion | flops 27525120 | bytes 6389760 | tf_op jit(solution)/shard_map/mul | solution.py:72
  51.8 9.9 %fusion.4 = (f32[3,16,128]{2,1,0:T(8,128)S(1)}, f32[3,16,128]{2,1,0:T(8,128)S(1)}, f32[16,128,128]{2,1,0:T(8,128)S(1)}, f32[3,16,128]{2,1,0:T(8,128)S(1)}, f32[3...) fusion(f32[16,128,128]{2,1,0:T(8,128)S(1)} %get-tuple-element.5, ...), kind=kLoop, calls=%fused_computation.8 | loop fusion | flops 31383552 | bytes 9879636 | tf_op jit(solution)/shard_map/reduce_sum | solution.py:74
  61.7 4.9 %fusion.167 = (f32[]{:T(128)}, f32[]{:T(128)}, f32[]{:T(128)}, f32[]{:T(128)}, f32[16,128,128]{2,1,0:T(8,128)S(1)}) fusion(f32[16,128,128]{2,1,0:T(8,128)S(1)} %get-tuple-element.459, f32[16,128]{1,0:T(8,128)S(1)} %bitcast.148, f32[16,128]{1,0:T(8,128)S(1)} %bitcast.145, f32[16,128]{1,0:T(8,128)S(1)} %bitcast.142, f32[16,128]{1,0:T(8,128)S(1)} %bitcast.130, ...), kind=kLoop, calls=%fused_computation.349 | loop fusion | flops 23855100 | bytes 4292624 | tf_op jit(solution)/shard_map/reduce_sum | solution.py:74
  66.6 7.0 %fusion.153 = (f32[]{:T(128)}, f32[]{:T(128)}, f32[]{:T(128)}, f32[]{:T(128)}, f32[]{:T(128)}, /*index=5*/f32[]{:T(128)}, f32[16,128,128]{2,1,0:T(8,128)S(1)}, f32[16,128,128]{2,1,0:T(8,128)S(1)}) fusion(f32[16,128,128]{2,1,0:T(8,128)S(1)} %get-tuple-element.460, f32[16,128]{1,0:T(8,128)S(1)} %bitcast.125, f32[16,128]{1,0:T(8,128)S(1)} %bitcast.122, ...), kind=kLoop, calls=%fused_computation.335 | loop fusion | flops 37224444 | bytes 6455320 | tf_op jit(solution)/shard_map/reduce_sum | solution.py:74
  73.6 4.6 %fusion.125 = (f32[]{:T(128)}, f32[]{:T(128)}, f32[]{:T(128)}, f32[]{:T(128)}, f32[16,128,128]{2,1,0:T(8,128)S(1)}) fusion(f32[16,128,128]{2,1,0:T(8,128)S(1)} %get-tuple-element.457, f32[16,128]{1,0:T(8,128)S(1)} %bitcast.192, f32[16,128]{1,0:T(8,128)S(1)} %bitcast.193, f32[16,128]{1,0:T(8,128)S(1)} %bitcast.194, f32[16,128]{1,0:T(8,128)S(1)} %bitcast.191, ...), kind=kLoop, calls=%fused_computation.307 | loop fusion | flops 23855100 | bytes 4292624 | tf_op jit(solution)/shard_map/reduce_sum | solution.py:74
  78.2 3.0 %fusion.22 = (f32[3,16,128]{2,1,0:T(8,128)S(1)}, f32[3,16,128]{2,1,0:T(8,128)S(1)}, f32[3,16,128]{2,1,0:T(8,128)S(1)}, f32[3,16,128]{2,1,0:T(8,128)S(1)}) fusion(f32[16,128,128]{2,1,0:T(8,128)S(1)} %get-tuple-element.491, f32[3,16,128]{2,1,0:T(8,128)S(1)} %bitcast.107, f32[3,16,128]{2,1,0:T(8,128)S(1)} %bitcast.82, f32[16,128,128]{2,1,0:T(8,128)S(1)} %get-tuple-element.499), kind=kLoop, calls=%fused_computation.38 | loop fusion | flops 7053312 | bytes 2244608 | tf_op jit(solution)/shard_map/reduce_sum | solution.py:74
  81.3 0.6 neg.108
  82.2 0.2 scatter-add.119
  82.4 0.8 fusion.319
  83.2 0.8 slice_add_fusion.16
  84.0 0.2 scatter-add.121
  84.3 0.2 scatter-add.125
  84.5 0.2 scatter-add.129
  84.8 5.0 %fusion.10 = (f32[3,16,128]{2,1,0:T(8,128)S(1)}, f32[3,16,128]{2,1,0:T(8,128)S(1)}, f32[3,16,128]{2,1,0:T(8,128)S(1)}, f32[3,16,128]{2,1,0:T(8,128)S(1)}, f32[3,...) fusion(f32[16,128,128]{2,1,0:T(8,128)S(1)} %get-tuple-element.498, f32[3]{0:T(128)S(1)} %copy-done.12, ...), kind=kLoop, calls=%fused_computation.18 | loop fusion | flops 11759616 | bytes 3366948 | tf_op jit(solution)/shard_map/reduce_sum | solution.py:74
  89.9 0.2 scatter-add.135
  90.2 0.2 scatter-add.139
  90.5 0.2 scatter-add.141
  90.8 0.2 scatter-add.145
  91.1 0.2 scatter-add.149
  91.4 0.4 collective-permute-start.3
  91.8 5.6 %collective-permute-done.3 = f32[3,3,5,1,128]{4,3,2,1,0:T(1,128)S(1)} collective-permute-done((f32[3,3,5,1,128]{4,3,2,1,0:T(1,128)S(1)}, f32[3,3,5,1,128]{4,3,2,1,0:T(1,128)S(1)}, u32[]{:S(2)}, u32[]{:S(2)}) %collective-permute-start.3) | collective-permute-done | bytes 23072 | tf_op jit(solution)/shard_map/ppermute | solution.py:18
  97.4 0.1 scatter-add.150
  97.6 0.1 collective-permute-start.4
  115.2 16.3 %all-reduce.1 = (f32[]{:T(128)}, f32[]{:T(128)}) all-reduce(f32[]{:T(128)S(6)} %add.995, f32[]{:T(128)S(6)} %add.982), channel_id=1, replica_groups=mesh['gx'=4,'gy'=2,'gz'=4] {'gy','gz'}, use_global_device_ids=true, to_apply=%region_75.0 | all-reduce | flops 2 | bytes 16 | tf_op jit(solution)/shard_map/psum | solution.py:122
  131.6 11.4 %all-reduce.2 = (f32[1]{0:T(128)}, f32[1]{0:T(128)}) all-reduce(f32[1]{0:T(128)} %bitcast.71, f32[1]{0:T(128)} %bitcast.70), channel_id=1, replica_groups=mesh['gx'=4,'gy'=2,'gz'=4] {'gx'}, use_global_device_ids=true, to_apply=%region_76.0 | all-reduce | flops 2 | bytes 16 | tf_op jit(solution)/shard_map/psum | solution.py:122
  143.0 1.9 %maximum_multiply_fusion = f32[2]{0:T(128)} fusion(f32[1]{0:T(128)} %get-tuple-element.487, f32[1]{0:T(128)} %get-tuple-element.488), kind=kLoop, calls=%fused_computation.665 | loop fusion | flops 4 | bytes 16 | tf_op jit(solution)/shard_map/mul | solution.py:132
  144.9 2.7 %collective-permute-done.5 = f32[3,1,4,2,128]{4,3,2,1,0:T(2,128)S(1)} collective-permute-done((f32[3,1,4,2,128]{4,3,2,1,0:T(2,128)S(1)}, f32[3,1,4,2,128]{4,3,2,1,0:T(2,128)S(1)}, u32[]{:S(2)}, u32[]{:S(2)}) %collective-permute-start.5) | collective-permute-done | bytes 12320 | tf_op jit(solution)/shard_map/ppermute | solution.py:18
  147.6 0.6 copy-done.3
  (101 shorter events, 1.4 us)
Async XLA Ops:
  0.6 16.4 %copy-start.5 = (f32[3]{0:T(128)S(1)}, f32[3]{0:T(128)}, u32[]{:S(2)}) copy-start(f32[3]{0:T(128)} %constant.879.clone) | copy-start | bytes 40
  0.6 16.4 %copy-start.13 = (f32[3]{0:T(128)S(1)}, f32[3]{0:T(128)}, u32[]{:S(2)}) copy-start(f32[3]{0:T(128)} %constant.880.clone) | copy-start | bytes 40
  0.7 16.4 %copy-start.14 = (f32[3]{0:T(128)S(1)}, f32[3]{0:T(128)}, u32[]{:S(2)}) copy-start(f32[3]{0:T(128)} %constant.883.clone) | copy-start | bytes 40
  0.7 16.4 %copy-start.6 = (f32[3]{0:T(128)S(1)}, f32[3]{0:T(128)}, u32[]{:S(2)}) copy-start(f32[3]{0:T(128)} %constant.886.clone) | copy-start | bytes 40
  0.7 16.4 %copy-start.15 = (f32[3]{0:T(128)S(1)}, f32[3]{0:T(128)}, u32[]{:S(2)}) copy-start(f32[3]{0:T(128)} %constant.890.clone) | copy-start | bytes 40
  0.7 16.4 %copy-start = (f32[3,2,4,2,128]{4,3,2,1,0:T(2,128)S(1)}, f32[3,2,4,2,128]{4,3,2,1,0:T(2,128)}, u32[]{:S(2)}) copy-start(f32[3,2,4,2,128]{4,3,2,1,0:T(2,128)} %param.82) | copy-start | bytes 73732
  4.5 5.5 %collective-permute-start = (f32[7,1,4,2,128]{4,3,2,1,0:T(2,128)S(1)}, f32[7,1,4,2,128]{4,3,2,1,0:T(2,128)S(1)}, u32[]{:S(2)}, u32[]{:S(2)}) collective-permute-start(f32[7,1,4,2,128]{4,3,2,1,0:T(2,128)S(1)} %slice.1661), channel_id=1, source_target_pairs={{0,24},{8,0},{16,8},{24,16},{1,25},{9,1},{17,9},{25,17},{2,26},{10... | collective-permute-start | bytes 86024 | tf_op jit(solution)/shard_map/ppermute | solution.py:18
  10.1 1.3 collective-permute-start.1
  11.4 5.5 %collective-permute-start.2 = (f32[7,3,5,1,128]{4,3,2,1,0:T(1,128)S(1)}, f32[7,3,5,1,128]{4,3,2,1,0:T(1,128)S(1)}, u32[]{:S(2)}, u32[]{:S(2)}) collective-permute-start(f32[7,3,5,1,128]{4,3,2,1,0:T(1,128)S(1)} %slice.1680), channel_id=1, source_target_pairs={{0,3},{1,0},{2,1},{3,2},{4,7},{5,4},{6,5},{7,6},{8,11},{9,8},{10,9... | collective-permute-start | bytes 161288 | tf_op jit(solution)/shard_map/ppermute | solution.py:18
  23.8 7.5 %copy-start.7 = (f32[3]{0:T(128)S(1)}, f32[3]{0:T(128)}, u32[]{:S(2)}) copy-start(f32[3]{0:T(128)} %constant.881.clone) | copy-start | bytes 40
  23.8 7.5 %copy-start.8 = (f32[3]{0:T(128)S(1)}, f32[3]{0:T(128)}, u32[]{:S(2)}) copy-start(f32[3]{0:T(128)} %constant.882.clone) | copy-start | bytes 40
  23.8 7.4 %copy-start.9 = (f32[3]{0:T(128)S(1)}, f32[3]{0:T(128)}, u32[]{:S(2)}) copy-start(f32[3]{0:T(128)} %constant.884.clone) | copy-start | bytes 40
  23.9 7.4 %copy-start.10 = (f32[3]{0:T(128)S(1)}, f32[3]{0:T(128)}, u32[]{:S(2)}) copy-start(f32[3]{0:T(128)} %constant.888.clone) | copy-start | bytes 40
  23.9 7.4 %copy-start.11 = (f32[3]{0:T(128)S(1)}, f32[3]{0:T(128)}, u32[]{:S(2)}) copy-start(f32[3]{0:T(128)} %constant.891.clone) | copy-start | bytes 40
  23.9 7.4 %copy-start.12 = (f32[3]{0:T(128)S(1)}, f32[3]{0:T(128)}, u32[]{:S(2)}) copy-start(f32[3]{0:T(128)} %constant.889.clone) | copy-start | bytes 40
  47.0 4.8 %copy-start.4 = (f32[3]{0:T(128)S(1)}, f32[3]{0:T(128)}, u32[]{:S(2)}) copy-start(f32[3]{0:T(128)} %constant.887.clone) | copy-start | bytes 40
  84.8 6.0 %copy-start.1 = (f32[3,16,128]{2,1,0:T(8,128)S(1)}, f32[3,16,128]{2,1,0:T(8,128)}, u32[]{:S(2)}) copy-start(f32[3,16,128]{2,1,0:T(8,128)} %get-tuple-element.462) | copy-start | bytes 73732
  84.8 6.0 %copy-start.2 = (f32[3,16,128]{2,1,0:T(8,128)S(1)}, f32[3,16,128]{2,1,0:T(8,128)}, u32[]{:S(2)}) copy-start(f32[3,16,128]{2,1,0:T(8,128)} %get-tuple-element.461) | copy-start | bytes 73732
  91.4 6.0 %collective-permute-start.3 = (f32[3,3,5,1,128]{4,3,2,1,0:T(1,128)S(1)}, f32[3,3,5,1,128]{4,3,2,1,0:T(1,128)S(1)}, u32[]{:S(2)}, u32[]{:S(2)}) collective-permute-start(f32[3,3,5,1,128]{4,3,2,1,0:T(1,128)S(1)} %slice.1705), channel_id=1, source_target_pairs={{0,1},{1,2},{2,3},{3,0},{4,5},{5,6},{6,7},{7,4},{8,9},{9,10},{10,1... | collective-permute-start | bytes 69128 | tf_op jit(solution)/shard_map/ppermute | solution.py:18
  97.6 45.4 %collective-permute-start.4 = (f32[3,3,1,2,128]{4,3,2,1,0:T(2,128)S(1)}, f32[3,3,1,2,128]{4,3,2,1,0:T(2,128)S(1)}, u32[]{:S(2)}, u32[]{:S(2)}) collective-permute-start(f32[3,3,1,2,128]{4,3,2,1,0:T(2,128)S(1)} %slice.1708), channel_id=1, source_target_pairs={{0,4},{4,0},{1,5},{5,1},{2,6},{6,2},{3,7},{7,3},{8,12},{12,8},{9,1... | collective-permute-start | bytes 27656 | tf_op jit(solution)/shard_map/ppermute | solution.py:18
  142.9 4.6 %collective-permute-start.5 = (f32[3,1,4,2,128]{4,3,2,1,0:T(2,128)S(1)}, f32[3,1,4,2,128]{4,3,2,1,0:T(2,128)S(1)}, u32[]{:S(2)}, u32[]{:S(2)}) collective-permute-start(f32[3,1,4,2,128]{4,3,2,1,0:T(2,128)S(1)} %slice.1711), channel_id=1, source_target_pairs={{0,8},{8,16},{16,24},{24,0},{1,9},{9,17},{17,25},{25,1},{2,10},{10... | collective-permute-start | bytes 36872 | tf_op jit(solution)/shard_map/ppermute | solution.py:18
  147.6 0.6 copy-start.3
